TPU v7x, 16 devices: a 4x2x1 block of a 4x4x8 slice. The times are simulated.
16 devices in a mesh: dp: 2 (over y, z), ctx: 8 (over x, core).
Axes of the slice: x: 4, y: 2, z: 1, core: 2. Of those that a mesh axis runs over, the one named last changes fastest.
The devices are a block of a 4x4x8 slice.
Arguments:
- queries: bfloat16 [64, 1024, 8, 128], P('dp', 'ctx'), parts along dimension 0
- keys: bfloat16 [64, 1024, 1, 128], P('dp', 'ctx'), parts along dimension 0
- values: bfloat16 [64, 1024, 1, 128], P('dp', 'ctx'), parts along dimension 0
- grad_out: bfloat16 [64, 1024, 8, 128], P('dp', 'ctx'), parts along dimension 0
Outputs:
- output 1: bfloat16 [64, 1024, 8, 128], P('dp', 'ctx'), parts along dimension 0
- output 2: bfloat16 [64, 1024, 8, 128], P('dp', 'ctx'), parts along dimension 0
- output 3: bfloat16 [64, 1024, 1, 128], P('dp', 'ctx'), parts along dimension 0
- output 4: bfloat16 [64, 1024, 1, 128], P('dp', 'ctx'), parts along dimension 0
There are 2 independent parts. A program takes and returns all parts, laid end to end along the dimension named above; each array names one.
All inputs are finite; a program needn't handle non-finite values.
Results may differ from a plain program's by a relative error of at most 0.00671496.
Values are sent between devices in bfloat16 or wider.
A program may use at most 768 MiB of HBM per device.

v0:
```python
import jax
import jax.numpy as jnp
from jax import lax
from jax.sharding import PartitionSpec as P

NEG_BIG = -1e30


def block_scores(q_heads, k_blk, q_start, k_start, scale):
    scores = jnp.einsum("bihgd,bjhd->bhgij", q_heads, k_blk, preferred_element_type=jnp.float32) * scale
    q_pos = q_start + jnp.arange(q_heads.shape[1])
    k_pos = k_start + jnp.arange(k_blk.shape[1])
    return jnp.where(q_pos[:, None] >= k_pos[None, :], scores, NEG_BIG)


def attend_forward(q_heads, k_all, v_all, dev_idx, scale):
    n_batch, c_len, n_kv, n_grp, d_head = q_heads.shape
    stat_shape = (n_batch, n_kv, n_grp, c_len)
    q_start = dev_idx * c_len

    def loop_body(key_idx, carry):
        m_run, l_run, acc_run = carry
        k_blk = lax.dynamic_index_in_dim(k_all, key_idx, 1, keepdims=False)
        v_blk = lax.dynamic_index_in_dim(v_all, key_idx, 1, keepdims=False)
        scores = block_scores(q_heads, k_blk, q_start, key_idx * c_len, scale)
        m_new = jnp.maximum(m_run, scores.max(axis=-1))
        rescale = jnp.exp(m_run - m_new)
        weights = jnp.exp(scores - m_new[..., None])
        l_new = l_run * rescale + weights.sum(axis=-1)
        acc_new = acc_run * rescale[..., None] + jnp.einsum("bhgij,bjhd->bhgid", weights.astype(jnp.bfloat16), v_blk, preferred_element_type=jnp.float32)
        return m_new, l_new, acc_new

    init_carry = (jnp.full(stat_shape, NEG_BIG, jnp.float32), jnp.zeros(stat_shape, jnp.float32), jnp.zeros(stat_shape + (d_head,), jnp.float32))
    m_fin, l_fin, acc_fin = lax.fori_loop(0, dev_idx + 1, loop_body, init_carry)
    out_heads = jnp.transpose((acc_fin / l_fin[..., None]).astype(jnp.bfloat16), (0, 3, 1, 2, 4))
    return out_heads, m_fin + jnp.log(l_fin)


def attend_backward(q_heads, do_heads, out_heads, lse_row, k_all, v_all, dev_idx, scale):
    c_len = q_heads.shape[1]
    q_start = dev_idx * c_len
    delta_row = jnp.einsum("bihgd,bihgd->bhgi", do_heads, out_heads, preferred_element_type=jnp.float32)

    def loop_body(key_idx, carry):
        dq_acc, dk_all, dv_all = carry
        k_blk = lax.dynamic_index_in_dim(k_all, key_idx, 1, keepdims=False)
        v_blk = lax.dynamic_index_in_dim(v_all, key_idx, 1, keepdims=False)
        scores = block_scores(q_heads, k_blk, q_start, key_idx * c_len, scale)
        weights = jnp.exp(scores - lse_row[..., None])
        dv_blk = jnp.einsum("bhgij,bihgd->bjhd", weights.astype(jnp.bfloat16), do_heads, preferred_element_type=jnp.float32)
        dp_blk = jnp.einsum("bihgd,bjhd->bhgij", do_heads, v_blk, preferred_element_type=jnp.float32)
        ds_half = (weights * (dp_blk - delta_row[..., None])).astype(jnp.bfloat16)
        dq_acc = dq_acc + jnp.einsum("bhgij,bjhd->bihgd", ds_half, k_blk, preferred_element_type=jnp.float32)
        dk_blk = jnp.einsum("bhgij,bihgd->bjhd", ds_half, q_heads, preferred_element_type=jnp.float32)
        dk_all = lax.dynamic_update_index_in_dim(dk_all, dk_blk, key_idx, 1)
        dv_all = lax.dynamic_update_index_in_dim(dv_all, dv_blk, key_idx, 1)
        return dq_acc, dk_all, dv_all

    acc_zero = jnp.zeros(k_all.shape, jnp.float32)
    init_carry = (jnp.zeros(q_heads.shape, jnp.float32), acc_zero, acc_zero)
    return lax.fori_loop(0, dev_idx + 1, loop_body, init_carry)


def solution(mesh):
    part_spec = P("dp", "ctx")

    def local_step(queries, keys, values, grad_out):
        n_batch, c_len, n_q, d_head = queries.shape
        n_kv = keys.shape[2]
        scale = d_head ** -0.5
        dev_idx = lax.axis_index("ctx")
        head_shape = (n_batch, c_len, n_kv, n_q // n_kv, d_head)
        q_heads = queries.reshape(head_shape)
        do_heads = grad_out.reshape(head_shape)
        k_all = lax.all_gather(keys, "ctx", axis=1)
        v_all = lax.all_gather(values, "ctx", axis=1)
        out_heads, lse_row = attend_forward(q_heads, k_all, v_all, dev_idx, scale)
        dq_acc, dk_all, dv_all = attend_backward(q_heads, do_heads, out_heads, lse_row, k_all, v_all, dev_idx, scale)
        dk_sum = lax.psum_scatter(dk_all, "ctx", scatter_dimension=1)
        dv_sum = lax.psum_scatter(dv_all, "ctx", scatter_dimension=1)
        attn_out = out_heads.reshape(n_batch, c_len, n_q, d_head)
        grad_q = (dq_acc * scale).astype(jnp.bfloat16).reshape(n_batch, c_len, n_q, d_head)
        grad_k = (dk_sum * scale).astype(jnp.bfloat16)
        grad_v = dv_sum.astype(jnp.bfloat16)
        return attn_out, grad_q, grad_k, grad_v

    return jax.shard_map(local_step, mesh=mesh, in_specs=(part_spec,) * 4, out_specs=(part_spec,) * 4, check_vma=False)
```

profile of v0, /device:TPU:113, one launch (start us, length us, event | category | flops | bytes accessed | tf_op | source)
XLA Modules:
  0.0 1199.9 jit_solution(7456167405128019228)
XLA Ops:
  7.2 0.1 all-gather.5.cloned.1.call-start
  7.2 0.7 all-gather.5.cloned.1.call-update
  8.0 0.1 all-gather.7.cloned.1.call-start
  8.0 0.7 all-gather.7.cloned.1.call-update
  8.8 0.1 reduce-scatter.5.cloned.1.call-start
  8.9 13.1 %copy_bitcast_fusion = (bf16[32,128,1,8,128]{4,1,3,0,2:T(8,128)(2,1)}, bf16[32,128,1,8,128]{4,1,3,0,2:T(8,128)(2,1)}) fusion(bf16[32,128,8,128]{3,2,1,0:T(8,128)(2,1)} %param.11, bf16[32,128,8,128]{3,2,1,0:T(8,128)(2,1)} %param.8), kind=kLoop, calls=%fused_computation.72 | loop fusion | bytes 33554432 | tf_op jit(solution)/shard_map/reshape | solution.py:74
  22.0 36.4 %all-gather.5.cloned.1.call-done = bf16[32,1024,1,128]{3,1,0,2:T(8,128)(2,1)} async-done(((bf16[32,128,1,128]{3,1,0,2:T(8,128)(2,1)}), bf16[32,1024,1,128]{3,1,0,2:T(8,128)(2,1)}) %all-gather.5.cloned.1.call-update) | async-done | bytes 8388624 | tf_op jit(solution)/shard_map/all_gather | solution.py:75
  58.4 10.5 copy.22
  68.9 36.7 %all-gather.7.cloned.1.call-done = bf16[32,1024,1,128]{3,1,0,2:T(8,128)(2,1)} async-done(((bf16[32,128,1,128]{3,1,0,2:T(8,128)(2,1)}), bf16[32,1024,1,128]{3,1,0,2:T(8,128)(2,1)}) %all-gather.7.cloned.1.call-update) | async-done | bytes 8388624 | tf_op jit(solution)/shard_map/all_gather | solution.py:76
  105.6 10.3 copy.23
  116.0 7.9 broadcast_in_dim.47
  123.8 82.6 %while.28 = (s32[]{:T(128)}, f32[32,1,8,128]{3,2,0,1:T(8,128)S(1)}, f32[32,1,8,128]{3,2,0,1:T(8,128)S(1)}, f32[32,1,8,128,128]{4,3,2,0,1:T(8,128)}, s32[]{:T(128...) while((s32[]{:T(128)}, f32[32,1,8,128]{3,2,0,1:T(8,128)S(1)}, ...), condition=%wide.region_3.4_spmd, body=%wide.region_0.3_spmd.sunk | while | flops 2202124544 | bytes 96536768 | solution.py:34
  124.0 0.1 broadcast_compare_fusion.4
  124.1 12.0 %fusion.83 = (f32[32,8,128]{2,1,0:T(8,128)S(1)}, f32[32,128,128,8]{2,1,3,0:T(8,128)}) fusion(pred[128,128]{0,1:T(8,128)(4,1)S(1)} %broadcast_compare_fusion.4, bf16[32,128,1,8,128]{4,1,3,0,2:T(8,128)(2,1)} %get-tuple-element.379, bf16[32,8,128,1,128]{4,2,0,3,1:T(8,128)(2,1)} %get-tuple-element.378, s32[]{:T(128)S(6)} %select_n.53), kind=kOutput, calls=%fused_computation.5.clone.1 | convolution fusion | flops 1086291968 | bytes 26361860 | tf_op jit(solution)/shard_map/while/body/bihgd,bjhd->bhgij/dot_general | solution.py:10
  136.2 10.2 fusion.85
  146.4 18.7 %bitcast_add_fusion.7 = f32[32,1,8,128,128]{4,3,2,0,1:T(8,128)} fusion(f32[32,1,8,128,128]{4,3,2,0,1:T(8,128)} %get-tuple-element.362, f32[32,128,128,8]{2,1,3,0:T(8,128)} %get-tuple-element.330, f32[32,8,128]{2,1,0:T(8,128)S(1)} %get-tuple-element.331, f32[32,8,128]{2,1,0:T(8,128)S(1)} %bitcast.228, ...), kind=kOutput, calls=%fused_computation.1.clone.1 | convolution fusion | flops 1098907648 | bytes 51658756 | tf_op jit(solution)/shard_map/while/body/bhgij,bjhd->bhgid/dot_general | solution.py:30
  165.1 0.1 bitcast_add_fusion.6
  165.2 0.1 broadcast_compare_fusion.4
  165.3 12.0 %fusion.83 = (f32[32,8,128]{2,1,0:T(8,128)S(1)}, f32[32,128,128,8]{2,1,3,0:T(8,128)}) fusion(pred[128,128]{0,1:T(8,128)(4,1)S(1)} %broadcast_compare_fusion.4, bf16[32,128,1,8,128]{4,1,3,0,2:T(8,128)(2,1)} %get-tuple-element.379, bf16[32,8,128,1,128]{4,2,0,3,1:T(8,128)(2,1)} %get-tuple-element.378, s32[]{:T(128)S(6)} %select_n.53), kind=kOutput, calls=%fused_computation.5.clone.1 | convolution fusion | flops 1086291968 | bytes 26361860 | tf_op jit(solution)/shard_map/while/body/bihgd,bjhd->bhgij/dot_general | solution.py:10
  177.4 10.2 fusion.85
  187.6 18.7 %bitcast_add_fusion.7 = f32[32,1,8,128,128]{4,3,2,0,1:T(8,128)} fusion(f32[32,1,8,128,128]{4,3,2,0,1:T(8,128)} %get-tuple-element.362, f32[32,128,128,8]{2,1,3,0:T(8,128)} %get-tuple-element.330, f32[32,8,128]{2,1,0:T(8,128)S(1)} %get-tuple-element.331, f32[32,8,128]{2,1,0:T(8,128)S(1)} %bitcast.228, ...), kind=kOutput, calls=%fused_computation.1.clone.1 | convolution fusion | flops 1098907648 | bytes 51658756 | tf_op jit(solution)/shard_map/while/body/bhgij,bjhd->bhgid/dot_general | solution.py:30
  206.3 0.1 bitcast_add_fusion.6
  206.4 0.6 copy.24
  207.0 20.8 %fusion.59 = (f32[32,8,128]{1,2,0:T(8,128)}, bf16[32,1,8,128,128]{4,2,3,0,1:T(8,128)(2,1)}) fusion(bf16[32,128,8,128]{3,2,1,0:T(8,128)(2,1)} %param.11, f32[32,8,128]{1,2,0:T(8,128)S(1)} %copy.24, f32[32,1,8,128,128]{4,3,2,0,1:T(8,128)} %get-tuple-element.119), kind=kLoop, calls=%fused_computation.67 | loop fusion | flops 25133056 | bytes 33816576
  227.8 2.2 copy.45
  230.0 7.8 broadcast_in_dim.49.clone
  237.8 7.9 broadcast_in_dim.49
  245.7 7.9 broadcast_in_dim.48
  253.5 128.4 %while.29 = (s32[]{:T(128)}, f32[32,128,1,8,128]{1,4,3,0,2:T(8,128)}, f32[32,8,128,1,128]{4,2,0,3,1:T(8,128)}, f32[32,8,128,1,128]{4,2,0,3,1:T(8,128)}, s32[]{:T...) while((s32[]{:T(128)}, ...), condition=%wide.region_5.6_spmd, body=%wide.region_4.5_spmd.sunk | while | flops 5414862848 | bytes 150391008 | solution.py:61
  253.5 0.1 broadcast_compare_fusion.5
  253.6 11.8 fusion.96
  265.4 13.2 %fusion.97 = bf16[32,1,8,128,128]{3,4,2,0,1:T(8,128)(2,1)} fusion(f32[32,128,128,8]{2,1,3,0:T(8,128)} %fusion.96, bf16[32,128,1,8,128]{4,1,3,0,2:T(8,128)(2,1)} %get-tuple-element.427, f32[32,8,128]{2,1,0:T(8,128)S(1)} %bitcast.238, f32[32,8,128]{2,1,0:T(8,128)S(1)} %bitcast.235, pred[128,128]{0,1:T(8,128)(4,1)S(1)} %broadcast_compare_fusion.5, ...), kind=kOutput, calls=%fused_computation.31.clone.1 | convolution fusion | flops 1098907648 | bytes 34881540 | tf_op jit(solution)/shard_map/while/body/bihgd,bjhd->bhgij/dot_general | solution.py:51
  278.6 13.1 %bitcast_dynamic-update-slice_fusion.5 = f32[32,8,128,1,128]{4,2,0,3,1:T(8,128)} fusion(f32[32,8,128,1,128]{4,2,0,3,1:T(8,128)} %get-tuple-element.404, s32[]{:T(128)S(6)} %select_n.56, bf16[32,128,1,8,128]{4,1,3,0,2:T(8,128)(2,1)} %get-tuple-element.427, f32[32,128,128,8]{2,1,3,0:T(8,128)} %fusion.96, f32[32,8,128]{2,1,0:T(8,128)S(1)} %bitcast.236, ...), kind=kOutput, calls=%fused_computation.50.clone.1 | convolution fusion | flops 1090519040 | bytes 27410436 | tf_op jit(solution)/shard_map/while/body/bhgij,bihgd->bjhd/dot_general | solution.py:50
  291.7 9.4 bitcast_dynamic-update-slice_fusion.4
  301.2 16.6 %bitcast_add_fusion.8 = f32[32,128,1,8,128]{1,4,3,0,2:T(8,128)} fusion(f32[32,128,1,8,128]{1,4,3,0,2:T(8,128)} %get-tuple-element.402, bf16[32,1,8,128,128]{3,4,2,0,1:T(8,128)(2,1)} %fusion.97, bf16[32,8,128,1,128]{4,2,0,3,1:T(8,128)(2,1)} %get-tuple-element.422, s32[]{:T(128)S(6)} %select_n.56), kind=kOutput, calls=%fused_computation.28.clone.1 | convolution fusion | flops 1077936128 | bytes 42991620 | tf_op jit(solution)/shard_map/while/body/bhgij,bjhd->bihgd/dot_general | solution.py:53
  317.7 0.1 broadcast_compare_fusion.5
  317.8 11.8 fusion.96
  329.6 13.2 %fusion.97 = bf16[32,1,8,128,128]{3,4,2,0,1:T(8,128)(2,1)} fusion(f32[32,128,128,8]{2,1,3,0:T(8,128)} %fusion.96, bf16[32,128,1,8,128]{4,1,3,0,2:T(8,128)(2,1)} %get-tuple-element.427, f32[32,8,128]{2,1,0:T(8,128)S(1)} %bitcast.238, f32[32,8,128]{2,1,0:T(8,128)S(1)} %bitcast.235, pred[128,128]{0,1:T(8,128)(4,1)S(1)} %broadcast_compare_fusion.5, ...), kind=kOutput, calls=%fused_computation.31.clone.1 | convolution fusion | flops 1098907648 | bytes 34881540 | tf_op jit(solution)/shard_map/while/body/bihgd,bjhd->bhgij/dot_general | solution.py:51
  342.8 13.1 %bitcast_dynamic-update-slice_fusion.5 = f32[32,8,128,1,128]{4,2,0,3,1:T(8,128)} fusion(f32[32,8,128,1,128]{4,2,0,3,1:T(8,128)} %get-tuple-element.404, s32[]{:T(128)S(6)} %select_n.56, bf16[32,128,1,8,128]{4,1,3,0,2:T(8,128)(2,1)} %get-tuple-element.427, f32[32,128,128,8]{2,1,3,0:T(8,128)} %fusion.96, f32[32,8,128]{2,1,0:T(8,128)S(1)} %bitcast.236, ...), kind=kOutput, calls=%fused_computation.50.clone.1 | convolution fusion | flops 1090519040 | bytes 27410436 | tf_op jit(solution)/shard_map/while/body/bhgij,bihgd->bjhd/dot_general | solution.py:50
  356.0 9.4 bitcast_dynamic-update-slice_fusion.4
  365.4 16.6 %bitcast_add_fusion.8 = f32[32,128,1,8,128]{1,4,3,0,2:T(8,128)} fusion(f32[32,128,1,8,128]{1,4,3,0,2:T(8,128)} %get-tuple-element.402, bf16[32,1,8,128,128]{3,4,2,0,1:T(8,128)(2,1)} %fusion.97, bf16[32,8,128,1,128]{4,2,0,3,1:T(8,128)(2,1)} %get-tuple-element.422, s32[]{:T(128)S(6)} %select_n.56), kind=kOutput, calls=%fused_computation.28.clone.1 | convolution fusion | flops 1077936128 | bytes 42991620 | tf_op jit(solution)/shard_map/while/body/bhgij,bjhd->bihgd/dot_general | solution.py:53
  381.9 0.1 reduce-scatter.5.cloned.1.call-update
  382.0 0.1 reduce-scatter.3.cloned.1.call-start
  382.1 0.6 reduce-scatter.3.cloned.1.call-update
  382.6 17.4 %copy.29 = f32[32,128,1,8,128]{4,3,1,0,2:T(8,128)} copy(f32[32,128,1,8,128]{1,4,3,0,2:T(8,128)} %get-tuple-element.122) | data formatting | bytes 33554432 | tf_op jit(solution)/shard_map/while | solution.py:61
  400.1 9.3 fusion.61
  409.4 691.0 %reduce-scatter.5.cloned.1.call-done = f32[32,1,128,1,128]{4,2,0,3,1:T(8,128)} async-done(((f32[32,8,128,1,128]{4,2,0,3,1:T(8,128)}), f32[32,1,128,1,128]{4,2,0,3,1:T(8,128)}) %reduce-scatter.5.cloned.1.call-update) | async-done | bytes 2097168 | tf_op jit(solution)/shard_map/reduce_scatter | solution.py:80
  1100.5 2.7 convert_bitcast_fusion
  1103.2 86.9 %reduce-scatter.3.cloned.1.call-done = f32[32,1,128,1,128]{4,2,0,3,1:T(8,128)} async-done(((f32[32,8,128,1,128]{4,2,0,3,1:T(8,128)}), f32[32,1,128,1,128]{4,2,0,3,1:T(8,128)}) %reduce-scatter.3.cloned.1.call-update) | async-done | bytes 2097168 | tf_op jit(solution)/shard_map/reduce_scatter | solution.py:79
  1190.1 2.9 fusion.62
  (11 shorter events, 0.2 us)
Async XLA Ops:
  7.2 51.2 %all-gather.5.cloned.1.call-start = ((), (), s32[]{:S(2)}) async-start(), calls=%async_computation.4 | async-start | bytes 9437184 | tf_op jit(solution)/shard_map/all_gather | solution.py:75
  8.0 97.7 %all-gather.7.cloned.1.call-start = ((), (), s32[]{:S(2)}) async-start(), calls=%async_computation.5 | async-start | bytes 9437184 | tf_op jit(solution)/shard_map/all_gather | solution.py:76
  8.8 1091.7 %reduce-scatter.5.cloned.1.call-start = ((), (), s32[]{:S(2)}) async-start(), calls=%async_computation.3 | async-start | bytes 18874368 | tf_op jit(solution)/shard_map/reduce_scatter | solution.py:80
  382.0 808.1 %reduce-scatter.3.cloned.1.call-start = ((), (), s32[]{:S(2)}) async-start(), calls=%async_computation.2 | async-start | bytes 18874368 | tf_op jit(solution)/shard_map/reduce_scatter | solution.py:79
Sparse Core Ops, SparseCore 0:
  9.6 48.7 all-gather.4
  59.9 45.6 all-gather.6
  382.1 718.2 reduce-scatter.4
  1102.7 87.3 reduce-scatter.2
where the time goes:
time: 1210 us; the launch traced here: 1200 us
  waiting for transfers between devices  853 us (70%)
  matrix products  190 us (16%)
  local copies, waits for them, and re-layouts  85.6 us (7%)
  other arithmetic  56.7 us (5%)
  between operations  14.2 us (1%)
    reduce_scatter x1, waiting for transfers between devices, local_step(): dv_sum = lax.psum_scatter(dv_all, 'ctx', scatter_dimension=1)  691 us
    reduce_scatter x1, waiting for transfers between devices, local_step(): dk_sum = lax.psum_scatter(dk_all, 'ctx', scatter_dimension=1)  86.9 us
    dot_general x4, matrix products, block_scores(): jnp.einsum('bihgd,bjhd->bhgij', q_heads, k_blk, preferred_element_type=jn...  47.6 us
    dot_general x2, matrix products, loop_body(): jnp.einsum('bhgij,bjhd->bhgid', weights.astype(jnp.bfloat16), v_blk, pref...  37.4 us
    all_gather x1, waiting for transfers between devices, local_step(): v_all = lax.all_gather(values, 'ctx', axis=1)  36.7 us
    all_gather x1, waiting for transfers between devices, local_step(): k_all = lax.all_gather(keys, 'ctx', axis=1)  36.4 us
    dot_general x2, matrix products, loop_body(): jnp.einsum('bhgij,bjhd->bihgd', ds_half, k_blk, preferred_element_type=jn...  33.1 us
    dot_general x2, matrix products, loop_body(): jnp.einsum('bihgd,bjhd->bhgij', do_heads, v_blk, preferred_element_type=j...  26.5 us
  transfers between devices with their start and end apart: 4, of which 4 were waited for; matrix products, arithmetic and copies ran while one was open for 4% of the time, Pallas kernels for 0%

commit v1 on v0

v1 whole, which is shorter than its diff:
```python
import functools
import math

import jax
import jax.numpy as jnp
from jax import lax
from jax.experimental import pallas as pl
from jax.experimental.pallas import tpu as pltpu
from jax.sharding import PartitionSpec as P

NEG_BIG = -1e30
CHUNK = 256
AHEAD = 4
FORWARD = 3
LAG = 2
NT = (((1,), (1,)), ((), ()))


def mm(a, b):
    return jnp.dot(a, b, preferred_element_type=jnp.float32)


def mm_nt(a, b):
    return lax.dot_general(a, b, NT, preferred_element_type=jnp.float32)


def attend(chip, t, grp, qd, kv, kvt, grads):
    c_len, d_head = kv.shape[-2:]
    pair = 2 * c_len
    rows = qd.shape[-2]
    scale = d_head ** -0.5
    k2 = scale * math.log2(math.e)
    n = chip + 1
    for j in range(n):
        kvt[j, 0] = kv[j, t, 0].reshape(pair, d_head).T
        kvt[j, 1] = kv[j, t, 1].reshape(pair, d_head).T
        grads[j, t] = jnp.zeros(grads.shape[2:], jnp.float32)
    toks = CHUNK // grp

    def chunk(r, _):
        rs = pl.ds(pl.multiple_of(r * CHUNK, CHUNK), CHUNK)
        qs = [qd[t, half, 0, rs] for half in range(2)]
        dos = [qd[t, half, 1, rs] for half in range(2)]
        pbs, dss = [], []
        for half in range(2):
            q, do = qs[half], dos[half]
            span = [pair] * chip + [c_len * (half + 1)]
            keys = [kv[j, t, 0].reshape(pair, d_head)[:span[j]] for j in range(n)]
            vals = [kv[j, t, 1].reshape(pair, d_head)[:span[j]] for j in range(n)]
            s = [mm_nt(k, q) for k in keys]
            dp = [mm_nt(v, do) for v in vals]
            tok = half * c_len + r * toks + lax.broadcasted_iota(jnp.int32, (1, CHUNK), 1) // grp
            key_pos = lax.broadcasted_iota(jnp.int32, (span[-1], CHUNK), 0)
            s[-1] = jnp.where(key_pos <= tok, s[-1], NEG_BIG)
            m = functools.reduce(jnp.maximum, [x.max(axis=0, keepdims=True) for x in s])
            mk = m * k2
            p = [jnp.exp2(x * k2 - mk) for x in s]
            rl = 1.0 / sum(x.sum(axis=0, keepdims=True) for x in p)
            p = [x * rl for x in p]
            pb = [x.astype(jnp.bfloat16) for x in p]
            o_t = sum(mm(kvt[j, 1, :, :span[j]], pb[j]) for j in range(n)).astype(jnp.bfloat16)
            delta = jnp.sum(do.T.astype(jnp.float32) * o_t.astype(jnp.float32), axis=0, keepdims=True)
            ds = [(x * (y - delta)).astype(jnp.bfloat16) for x, y in zip(p, dp)]
            dq_t = sum(mm(kvt[j, 0, :, :span[j]], ds[j]) for j in range(n)) * scale
            qd[t, half, 0, rs] = o_t.T
            qd[t, half, 1, rs] = dq_t.astype(jnp.bfloat16).T
            pbs.append(pb)
            dss.append(ds)
        for j in range(n):
            if j < chip:
                grads[j, t, 0] += mm(dss[0][j], qs[0]) + mm(dss[1][j], qs[1])
                grads[j, t, 1] += mm(pbs[0][j], dos[0]) + mm(pbs[1][j], dos[1])
            else:
                grads[j, t, 0] += mm(dss[1][j], qs[1])
                grads[j, t, 1] += mm(pbs[1][j], dos[1])
                grads[j, t, 0, :c_len] += mm(dss[0][j], qs[0])
                grads[j, t, 1, :c_len] += mm(pbs[0][j], dos[0])
        return 0

    lax.fori_loop(0, rows // CHUNK, chunk, 0)


def run_chip(chip, n_chip, grp, q_ref, do_ref, kv_ref, odq_ref, dkv_ref, qd, kv, kvt, grads, inbox,
             load_sem, pair_send, pair_recv, kv_send, kv_recv, fwd_send, sum_send, sum_recv,
             out_sem, out_send, out_recv, g_sem, g_send, g_recv):
    nb = qd.shape[0]
    c_len, d_head = kv.shape[-2:]
    scale = d_head ** -0.5
    core = lax.axis_index("ctx") % 2
    last = n_chip - 1
    targets = []
    if chip < last:
        targets.append(chip + 1)
    if chip == 0 and last > 1:
        targets.append(last)

    def dev(to_chip, to_core):
        return {"ctx": 2 * to_chip + to_core}

    def remote(src, dst, send, recv, to):
        return pltpu.make_async_remote_copy(src_ref=src, dst_ref=dst, send_sem=send, recv_sem=recv, device_id=to,
                                            device_id_type=pl.DeviceIdType.MESH)

    def loads(t):
        b = core * nb + t
        return [pltpu.make_async_copy(q_ref.at[b], qd.at[t, core, 0], load_sem.at[0, t]),
                pltpu.make_async_copy(do_ref.at[b], qd.at[t, core, 1], load_sem.at[1, t]),
                pltpu.make_async_copy(kv_ref.at[b], kv.at[chip, t, :, core], load_sem.at[2, t])]

    def pair_copies(t, half):
        b = (1 - core) * nb + t
        to = dev(chip, 1 - core)
        return [remote(q_ref.at[b], qd.at[t, half, 0], pair_send.at[0, t], pair_recv.at[0, t], to),
                remote(do_ref.at[b], qd.at[t, half, 1], pair_send.at[1, t], pair_recv.at[1, t], to),
                remote(kv_ref.at[b], kv.at[chip, t, :, half], pair_send.at[2, t], pair_recv.at[2, t], to)]

    def kv_pushes(t):
        out = []
        for i, to_chip in enumerate(targets):
            for other in range(2):
                plane = core if other == 0 else 1 - core
                out.append(remote(kv_ref.at[plane * nb + t], kv.at[chip, t, :, core], kv_send.at[i, other, t],
                                  kv_recv.at[chip, core, t], dev(to_chip, plane)))
        return out

    def direct(src):
        return src == chip - 1 or (src == 0 and chip == last)

    def kv_wait(src, t):
        if direct(src):
            for half in range(2):
                remote(kv_ref.at[0], kv.at[src, t, :, half], kv_send.at[0, 0, t], kv_recv.at[src, half, t],
                       dev(chip, 1 - core)).wait_recv()
        else:
            remote(kv.at[src, t], kv.at[src, t], fwd_send.at[0, t], kv_recv.at[src, 0, t], dev(chip, 1 - core)).wait_recv()

    fwd_srcs = [s for s in range(chip) if chip < last and not (s == 0 and chip + 1 == last)]

    def forward(i, t):
        src = fwd_srcs[i]
        return remote(kv.at[src, t], kv.at[src, t], fwd_send.at[i, t], kv_recv.at[src, 0, t], dev(chip + 1, core))

    def issue(t):
        for c in loads(t) + pair_copies(t, core) + kv_pushes(t):
            c.start()

    def issue_forward(t):
        for i, src in enumerate(fwd_srcs):
            kv_wait(src, t)
            forward(i, t).start()

    def send_sum(d, t):
        if chip == last and d == 0 and last > 1:
            to_chip, slot = 0, 0
        else:
            to_chip = chip - 1
            slot = 1 if d == to_chip else 0
        return remote(grads.at[d, t], inbox.at[slot, t], sum_send.at[d, t], sum_recv.at[slot, t], dev(to_chip, core))

    def inbox_wait(slot, t):
        remote(inbox.at[slot, t], inbox.at[slot, t], sum_send.at[0, t], sum_recv.at[slot, t],
               dev(chip, 1 - core)).wait_recv()

    merged = [d for d in range(chip) if chip < last and not (d == 0 and chip + 1 == last)]
    unmerged = [d for d in range(chip) if d not in merged]
    n_own = 0 if chip == last else (2 if (chip == 0 and last > 1) else 1)

    def outs(t):
        b = core * nb + t
        return [pltpu.make_async_copy(qd.at[t, core], odq_ref.at[b], out_sem.at[t]),
                remote(qd.at[t, 1 - core], odq_ref.at[b], out_send.at[t], out_recv.at[t], dev(chip, 1 - core))]

    def grad_outs(t):
        b = core * nb + t
        return [pltpu.make_async_copy(kv.at[chip, t, :, core], dkv_ref.at[b], g_sem.at[t]),
                remote(kv.at[chip, t, :, 1 - core], dkv_ref.at[b], g_send.at[t], g_recv.at[t], dev(chip, 1 - core))]

    def reduce_step(t):
        for d in merged:
            inbox_wait(0, t)
            grads[d, t] += inbox[0, t]
            send_sum(d, t).start()
        total = grads[chip, t]
        if n_own >= 1:
            inbox_wait(1, t)
            total = total + inbox[1, t]
        if n_own == 2:
            inbox_wait(0, t)
            total = total + inbox[0, t]
        block = (2, c_len, d_head)
        kv[chip, t, 0] = (total[0] * scale).astype(jnp.bfloat16).reshape(block)
        kv[chip, t, 1] = total[1].astype(jnp.bfloat16).reshape(block)
        for c in grad_outs(t):
            c.start()

    lag = LAG * (last - chip)

    def prologue(t, _):
        issue(t)
        return 0

    lax.fori_loop(0, AHEAD, prologue, 0)
    if fwd_srcs:
        def fwd_prologue(t, _):
            issue_forward(t)
            return 0
        lax.fori_loop(0, FORWARD, fwd_prologue, 0)

    def step(t, _):
        @pl.when(t + AHEAD < nb)
        def _():
            issue(t + AHEAD)
        if fwd_srcs:
            @pl.when(t + FORWARD < nb)
            def _():
                issue_forward(t + FORWARD)
        for c in loads(t):
            c.wait()
        for c in pair_copies(t, 1 - core):
            c.wait_recv()
        for src in range(chip):
            if src not in fwd_srcs:
                kv_wait(src, t)
        attend(chip, t, grp, qd, kv, kvt, grads)
        for c in outs(t):
            c.start()
        for d in unmerged[::-1]:
            send_sum(d, t).start()
        @pl.when(t >= lag)
        def _():
            reduce_step(t - lag)
        return 0

    lax.fori_loop(0, nb, step, 0)

    def tail(t, _):
        reduce_step(t)
        return 0

    if lag:
        lax.fori_loop(nb - lag, nb, tail, 0)

    def drain(t, _):
        for c in pair_copies(t, core) + kv_pushes(t):
            c.wait_send()
        for i in range(len(fwd_srcs)):
            forward(i, t).wait_send()
        for d in range(chip):
            send_sum(d, t).wait_send()
        b = (1 - core) * nb + t
        for local, away in (outs(t), grad_outs(t)):
            local.wait()
            away.wait_send()
        remote(qd.at[t, core], odq_ref.at[b], out_send.at[t], out_recv.at[t], dev(chip, 1 - core)).wait_recv()
        remote(kv.at[chip, t, :, core], dkv_ref.at[b], g_send.at[t], g_recv.at[t], dev(chip, 1 - core)).wait_recv()
        return 0

    lax.fori_loop(0, nb, drain, 0)


def kernel(n_chip, grp, *refs):
    me = lax.axis_index("ctx")
    barrier = pltpu.get_barrier_semaphore()
    for i in range(1, 2 * n_chip):
        pl.semaphore_signal(barrier, inc=1, device_id={"ctx": lax.rem(me + i, 2 * n_chip)},
                            device_id_type=pl.DeviceIdType.MESH)
    pl.semaphore_wait(barrier, 2 * n_chip - 1)
    for chip in range(n_chip):
        @pl.when(me // 2 == chip)
        def _():
            run_chip(chip, n_chip, grp, *refs)


def solution(mesh):
    part_spec = P("dp", "ctx")
    n_chip = mesh.shape["ctx"] // 2

    def local_step(queries, keys, values, grad_out):
        n_batch, c_len, n_q, d_head = queries.shape
        rows = c_len * n_q
        nb = n_batch // 2
        q = queries.reshape(n_batch, rows, d_head)
        do = grad_out.reshape(n_batch, rows, d_head)
        kv = jnp.stack([keys.reshape(n_batch, c_len, d_head), values.reshape(n_batch, c_len, d_head)], axis=1)
        dma = pltpu.SemaphoreType.DMA
        any_spec = pl.BlockSpec(memory_space=pl.ANY)
        pairs = n_chip
        flops = 2 * nb * 2 * rows * n_chip * 2 * c_len * d_head * 6
        odq, dkv = pl.pallas_call(
            functools.partial(kernel, n_chip, n_q),
            in_specs=[any_spec] * 3,
            out_specs=[any_spec] * 2,
            out_shape=[jax.ShapeDtypeStruct((n_batch, 2, rows, d_head), jnp.bfloat16),
                       jax.ShapeDtypeStruct((n_batch, 2, c_len, d_head), jnp.bfloat16)],
            scratch_shapes=[
                pltpu.VMEM((nb, 2, 2, rows, d_head), jnp.bfloat16),
                pltpu.VMEM((pairs, nb, 2, 2, c_len, d_head), jnp.bfloat16),
                pltpu.VMEM((pairs, 2, d_head, 2 * c_len), jnp.bfloat16),
                pltpu.VMEM((pairs, nb, 2, 2 * c_len, d_head), jnp.float32),
                pltpu.VMEM((2, nb, 2, 2 * c_len, d_head), jnp.float32),
                dma((3, nb)), dma((3, nb)), dma((3, nb)),
                dma((2, 2, nb)), dma((pairs, 2, nb)), dma((max(pairs - 2, 1), nb)),
                dma((pairs, nb)), dma((2, nb)),
                dma((nb,)), dma((nb,)), dma((nb,)),
                dma((nb,)), dma((nb,)), dma((nb,)),
            ],
            compiler_params=pltpu.CompilerParams(vmem_limit_bytes=67043328, collective_id=0, has_side_effects=True),
            cost_estimate=pl.CostEstimate(flops=flops, bytes_accessed=4 * q.size * 2, transcendentals=0),
        )(q, do, kv)
        shape, kv_shape = queries.shape, keys.shape
        return (odq[:, 0].reshape(shape), odq[:, 1].reshape(shape),
                dkv[:, 0].reshape(kv_shape), dkv[:, 1].reshape(kv_shape))

    return jax.shard_map(local_step, mesh=mesh, in_specs=(part_spec,) * 4, out_specs=(part_spec,) * 4, check_vma=False)
```

time: 1210 us -> 248 us (0.20)
  waiting for transfers between devices: 853 us -> 0 us
  Pallas kernels: 0 us -> 225 us
  matrix products: 190 us -> 0 us
  local copies, waits for them, and re-layouts: 85.6 us -> 13.4 us
  other arithmetic: 56.7 us -> 3.07 us
  between operations: 14.2 us -> 0.65 us
    reduce_scatter x2 -> x0, waiting for transfers between devices: 778 us -> none  [the longest x1 691 us: local_step(): dv_sum = lax.psum_scatter(dv_all, 'ctx', scatter_dimension=1)]
    pallas_call x0 -> x1, Pallas kernels: none -> 225 us  [local_step(): pl.pallas_call(functools.partial(kernel, n_chip, n_q), in_specs=[any_spec...]
    dot_general x14 -> x0, matrix products: 190 us -> none  [the longest x4 47.6 us: block_scores(): jnp.einsum('bihgd,bjhd->bhgij', q_heads, k_blk, preferred_element_type=jn...]
    all_gather x2 -> x0, waiting for transfers between devices: 73.1 us -> none  [the longest x1 36.7 us: local_step(): v_all = lax.all_gather(values, 'ctx', axis=1)]
    while x5 -> x0, local copies, waits for them, and re-layouts: 38.3 us -> none  [the longest x2 20.8 us: attend_forward(): m_fin, l_fin, acc_fin = lax.fori_loop(0, dev_idx + 1, loop_body, init_carry)]
    broadcast_in_dim x6 -> x0, local copies, waits for them, and re-layouts: 31.4 us -> none  [the longest x2 15.7 us: attend_backward(): acc_zero = jnp.zeros(k_all.shape, jnp.float32)]
    unnamed x1 -> x0, other arithmetic: 20.8 us -> none
    reduce_sum x2 -> x0, other arithmetic: 20.4 us -> none  [loop_body(): l_new = l_run * rescale + weights.sum(axis=-1)]
  transfers between devices with their start and end apart: 4 -> 0, of which waited for: 4 -> 0; matrix products, arithmetic and copies ran while one was open for 4% -> 0% of each run, Pallas kernels for 0% -> 0%
where the time goes in v1:
time: 248 us; the launch traced here: 243 us
  Pallas kernels  225 us (91%)
  local copies, waits for them, and re-layouts  13.4 us (5%)
  other arithmetic  3.07 us (1%)
    pallas_call x1, Pallas kernels, local_step(): pl.pallas_call(functools.partial(kernel, n_chip, n_q), in_specs=[any_spec...  225 us
    another operation x1, local copies, waits for them, and re-layouts, local_step(): odq[:, 1].reshape(shape)  11.8 us

profile of v1, /device:TPU:113, one launch (start us, length us, event | category | flops | bytes accessed | tf_op | source)
XLA Modules:
  0.0 242.6 jit_solution(18078735840064026027)
XLA Ops:
  0.6 3.1 %pad_maximum_fusion.refs_2_ = bf16[32,2,128,128]{3,2,1,0:T(8,128)(2,1)} fusion(bf16[32,1,128,128]{3,2,1,0:T(8,128)(2,1)} %bitcast.16, bf16[32,1,128,128]{3,2,1,0:T(8,128)(2,1)} %bitcast.17), kind=kLoop, calls=%fused_computation.2 | loop fusion | flops 1048576 | bytes 4194304 | tf_op jit(solution)/shard_map/stack | solution.py:284
  3.7 225.5 %shard_map.75 = (bf16[32,2,1024,128]{3,2,1,0:T(8,128)(2,1)}, bf16[32,2,128,128]{3,2,1,0:T(8,128)(2,1)}) custom-call(bf16[32,1024,128]{2,1,0:T(8,128)(2,1)} %bitcast.18, bf16[32,1024,128]{2,1,0:T(8,128)(2,1)} %bitcast.19, bf16[32,2,128,128]{3,2,1,0:T(8,128)(2,1)} %pad_maximum_fusion.refs_2_), custom_call_target="tpu_custom_call" | custom-call | flops 51539607552 | bytes 33554432 | tf_op jit(solution)/shard_map/pallas_call | solution.py:289
  229.2 0.0 copy-start
  229.2 11.8 %slice_bitcast_fusion = (bf16[32,128,8,128]{3,2,1,0:T(8,128)(2,1)}, bf16[32,128,8,128]{3,2,1,0:T(8,128)(2,1)}) fusion(bf16[32,2,1024,128]{3,2,1,0:T(8,128)(2,1)} %get-tuple-element.6), kind=kLoop, calls=%fused_computation | loop fusion | bytes 33554432 | tf_op jit(solution)/shard_map/reshape;squeeze | solution.py:311
  241.0 0.0 copy-done
  241.0 1.6 slice_bitcast_fusion.2
Async XLA Ops:
  229.2 11.8 %copy-start = (bf16[32,2,128,128]{3,2,1,0:T(8,128)(2,1)S(1)}, bf16[32,2,128,128]{3,2,1,0:T(8,128)(2,1)}, u32[]{:S(2)}) copy-start(bf16[32,2,128,128]{3,2,1,0:T(8,128)(2,1)} %get-tuple-element.7) | copy-start | bytes 6291460

commit v2 on v1

--- a/solution.py
+++ b/solution.py
@@ -9,10 +9,10 @@
 from jax.sharding import PartitionSpec as P
 
 NEG_BIG = -1e30
-CHUNK = 256
-AHEAD = 4
-FORWARD = 3
-LAG = 2
+CHUNK = 512
+EARLY = 2
+AHEAD = 3
+FORWARD = 2
 NT = (((1,), (1,)), ((), ()))
 
 
@@ -24,64 +24,117 @@
     return lax.dot_general(a, b, NT, preferred_element_type=jnp.float32)
 
 
-def attend(chip, t, grp, qd, kv, kvt, grads):
+def grad_parts(chip, half, t, bufs, grads):
+    pbs, dss, rows_buf = bufs
+    c_len = grads.shape[3] // 2
+
+    def part(j, which, buf):
+        span = slice(None) if half or j < chip else slice(0, c_len)
+
+        def run():
+            grads[j, t, which, span] += mm(buf[half, j, span], rows_buf[half, which])
+        return run
+
+    return [part(j, which, buf) for j in range(chip + 1) for which, buf in ((1, pbs), (0, dss))]
+
+
+def softmax_part(chip, half, r, t, grp, qd, kv, kvt, bufs, fill):
+    pbs, dss, rows_buf = bufs
     c_len, d_head = kv.shape[-2:]
     pair = 2 * c_len
-    rows = qd.shape[-2]
     scale = d_head ** -0.5
     k2 = scale * math.log2(math.e)
     n = chip + 1
+    fill = list(fill)
+    rs = pl.ds(pl.multiple_of(r * CHUNK, CHUNK), CHUNK)
+    q = qd[t, half, 0, rs]
+    do = qd[t, half, 1, rs]
+    rows_buf[half, 0] = q
+    rows_buf[half, 1] = do
+    span = [pair] * chip + [c_len * (half + 1)]
+    tops = [pair * j for j in range(n)]
+    n_key = sum(span)
+    keys = kv[:n, t, 0].reshape(n * pair, d_head)[:n_key]
+    vals = kv[:n, t, 1].reshape(n * pair, d_head)[:n_key]
+    s_all = mm_nt(keys, q)
+    s = [s_all[a:a + w] for a, w in zip(tops, span)]
+    tok = half * c_len + r * (CHUNK // grp) + lax.broadcasted_iota(jnp.int32, (1, CHUNK), 1) // grp
+    key_pos = lax.broadcasted_iota(jnp.int32, (span[-1], CHUNK), 0)
+    s[-1] = jnp.where(key_pos <= tok, s[-1], NEG_BIG)
+    m = functools.reduce(jnp.maximum, [x.max(axis=0, keepdims=True) for x in s])
+    mk = m * k2
+    p = []
+    l = 0.0
     for j in range(n):
+        parts = []
+        for a in range(0, span[j], c_len):
+            x = jnp.exp2(s[j][a:a + c_len] * k2 - mk)
+            l = l + x.sum(axis=0, keepdims=True)
+            parts.append(x)
+            if fill:
+                fill.pop(0)()
+        p.append(parts)
+    for step in fill:
+        step()
+    rl = 1.0 / l
+    o_t = None
+    for j in range(n):
+        for i, x in enumerate(p[j]):
+            pbs[half, j, i * c_len:(i + 1) * c_len] = (x * rl).astype(jnp.bfloat16)
+        part = mm(kvt[j, 1, :, :span[j]], pbs[half, j, :span[j]])
+        o_t = part if o_t is None else o_t + part
+    dps = [mm_nt(vals[a:a + w], do) for a, w in list(zip(tops, span))[:EARLY]]
+    o_t = o_t.astype(jnp.bfloat16)
+    delta = jnp.sum(do.T.astype(jnp.float32) * o_t.astype(jnp.float32), axis=0, keepdims=True)
+    dq_t = None
+    for j in range(n):
+        if j + EARLY < n:
+            a = tops[j + EARLY]
+            dps.append(mm_nt(vals[a:a + span[j + EARLY]], do))
+        for i, x in enumerate(p[j]):
+            at = slice(i * c_len, (i + 1) * c_len)
+            dss[half, j, at] = (x * rl * (dps[j][at] - delta)).astype(jnp.bfloat16)
+        part = mm(kvt[j, 0, :, :span[j]], dss[half, j, :span[j]])
+        dq_t = part if dq_t is None else dq_t + part
+    qd[t, half, 0, rs] = o_t.T
+    qd[t, half, 1, rs] = (dq_t * scale).astype(jnp.bfloat16).T
+
+
+def attend(chip, t, grp, qd, kv, kvt, grads, bufs, send_now):
+    c_len, d_head = kv.shape[-2:]
+    pair = 2 * c_len
+    nb = qd.shape[0]
+    for j in range(chip + 1):
         kvt[j, 0] = kv[j, t, 0].reshape(pair, d_head).T
         kvt[j, 1] = kv[j, t, 1].reshape(pair, d_head).T
         grads[j, t] = jnp.zeros(grads.shape[2:], jnp.float32)
-    toks = CHUNK // grp
 
     def chunk(r, _):
-        rs = pl.ds(pl.multiple_of(r * CHUNK, CHUNK), CHUNK)
-        qs = [qd[t, half, 0, rs] for half in range(2)]
-        dos = [qd[t, half, 1, rs] for half in range(2)]
-        pbs, dss = [], []
-        for half in range(2):
-            q, do = qs[half], dos[half]
-            span = [pair] * chip + [c_len * (half + 1)]
-            keys = [kv[j, t, 0].reshape(pair, d_head)[:span[j]] for j in range(n)]
-            vals = [kv[j, t, 1].reshape(pair, d_head)[:span[j]] for j in range(n)]
-            s = [mm_nt(k, q) for k in keys]
-            dp = [mm_nt(v, do) for v in vals]
-            tok = half * c_len + r * toks + lax.broadcasted_iota(jnp.int32, (1, CHUNK), 1) // grp
-            key_pos = lax.broadcasted_iota(jnp.int32, (span[-1], CHUNK), 0)
-            s[-1] = jnp.where(key_pos <= tok, s[-1], NEG_BIG)
-            m = functools.reduce(jnp.maximum, [x.max(axis=0, keepdims=True) for x in s])
-            mk = m * k2
-            p = [jnp.exp2(x * k2 - mk) for x in s]
-            rl = 1.0 / sum(x.sum(axis=0, keepdims=True) for x in p)
-            p = [x * rl for x in p]
-            pb = [x.astype(jnp.bfloat16) for x in p]
-            o_t = sum(mm(kvt[j, 1, :, :span[j]], pb[j]) for j in range(n)).astype(jnp.bfloat16)
-            delta = jnp.sum(do.T.astype(jnp.float32) * o_t.astype(jnp.float32), axis=0, keepdims=True)
-            ds = [(x * (y - delta)).astype(jnp.bfloat16) for x, y in zip(p, dp)]
-            dq_t = sum(mm(kvt[j, 0, :, :span[j]], ds[j]) for j in range(n)) * scale
-            qd[t, half, 0, rs] = o_t.T
-            qd[t, half, 1, rs] = dq_t.astype(jnp.bfloat16).T
-            pbs.append(pb)
-            dss.append(ds)
-        for j in range(n):
-            if j < chip:
-                grads[j, t, 0] += mm(dss[0][j], qs[0]) + mm(dss[1][j], qs[1])
-                grads[j, t, 1] += mm(pbs[0][j], dos[0]) + mm(pbs[1][j], dos[1])
-            else:
-                grads[j, t, 0] += mm(dss[1][j], qs[1])
-                grads[j, t, 1] += mm(pbs[1][j], dos[1])
-                grads[j, t, 0, :c_len] += mm(dss[0][j], qs[0])
-                grads[j, t, 1, :c_len] += mm(pbs[0][j], dos[0])
+        before = jnp.where(r == 0, jnp.maximum(t - 1, 0), t)
+        softmax_part(chip, 0, r, t, grp, qd, kv, kvt, bufs, grad_parts(chip, 1, before, bufs, grads))
+
+        @pl.when((r == 0) & (t >= 1))
+        def _():
+            send_now(t - 1)
+
+        @pl.when(t < nb)
+        def _():
+            softmax_part(chip, 1, r, t, grp, qd, kv, kvt, bufs, grad_parts(chip, 0, t, bufs, grads))
         return 0
 
-    lax.fori_loop(0, rows // CHUNK, chunk, 0)
-
-
-def run_chip(chip, n_chip, grp, q_ref, do_ref, kv_ref, odq_ref, dkv_ref, qd, kv, kvt, grads, inbox,
-             load_sem, pair_send, pair_recv, kv_send, kv_recv, fwd_send, sum_send, sum_recv,
+    lax.fori_loop(0, qd.shape[-2] // CHUNK, chunk, 0)
+
+
+NOW = {0: ((), ()), 1: (((0, 0, 1),), ()), 2: (((0, 3, 0),), ((1, 1, 1), (0, 1, 0))),
+       3: (((1, 2, 0), (2, 2, 1)), ((1, 0, 2), (0, 0, 0), (2, 2, 1)))}
+MERGED = {0: (None, None), 1: (None, (0, 0, 1)), 2: ((1, 1, 1), None), 3: ((0, 0, 0), None)}
+OWN_SLOTS = {0: (1, 0), 1: (1,), 2: (1,), 3: ()}
+LAGS = {0: 7, 1: 5, 2: 3, 3: 3}
+
+
+def run_chip(chip, n_chip, grp, q_ref, do_ref, kv_ref, odq_ref, dkv_ref, qd, kv, kvt, grads, inbox, relay,
+             pbs, dss, rows_buf, load_sem, pair_send, pair_recv, kv_send, kv_recv, fwd_send, sum_send, sum_recv,
+             relay_send, relay_recv,
              out_sem, out_send, out_recv, g_sem, g_send, g_recv):
     nb = qd.shape[0]
     c_len, d_head = kv.shape[-2:]
@@ -149,21 +202,26 @@
             kv_wait(src, t)
             forward(i, t).start()
 
-    def send_sum(d, t):
-        if chip == last and d == 0 and last > 1:
-            to_chip, slot = 0, 0
+    def send_sum(route, t):
+        d, to_chip, slot = route
+        if slot == 2:
+            dst, recv = relay.at[t // 2], relay_recv.at[t // 2]
         else:
-            to_chip = chip - 1
-            slot = 1 if d == to_chip else 0
-        return remote(grads.at[d, t], inbox.at[slot, t], sum_send.at[d, t], sum_recv.at[slot, t], dev(to_chip, core))
+            dst, recv = inbox.at[slot, t], sum_recv.at[slot, t]
+        return remote(grads.at[d, t], dst, sum_send.at[d, t], recv, dev(to_chip, core))
+
+    def relay_on(t):
+        u = t // 2
+        return remote(relay.at[u], relay.at[u], relay_send.at[u], relay_recv.at[u], dev(1, core))
 
     def inbox_wait(slot, t):
         remote(inbox.at[slot, t], inbox.at[slot, t], sum_send.at[0, t], sum_recv.at[slot, t],
                dev(chip, 1 - core)).wait_recv()
 
-    merged = [d for d in range(chip) if chip < last and not (d == 0 and chip + 1 == last)]
-    unmerged = [d for d in range(chip) if d not in merged]
-    n_own = 0 if chip == last else (2 if (chip == 0 and last > 1) else 1)
+    def by_parity(t, even, odd):
+        for parity, body in enumerate((even, odd)):
+            if body is not None:
+                pl.when(t % 2 == parity)(body)
 
     def outs(t):
         b = core * nb + t
@@ -175,25 +233,47 @@
         return [pltpu.make_async_copy(kv.at[chip, t, :, core], dkv_ref.at[b], g_sem.at[t]),
                 remote(kv.at[chip, t, :, 1 - core], dkv_ref.at[b], g_send.at[t], g_recv.at[t], dev(chip, 1 - core))]
 
+    def send_now(t):
+        def body(routes):
+            def start():
+                for route in routes:
+                    send_sum(route, t).start()
+            return start if routes else None
+        by_parity(t, *map(body, NOW[chip]))
+
+    def merge(t):
+        def body(route):
+            def pass_on():
+                inbox_wait(0, t)
+                grads[route[0], t] += inbox[0, t]
+                send_sum(route, t).start()
+            return pass_on if route else None
+        by_parity(t, *map(body, MERGED[chip]))
+        if chip < 2:
+            def relayed():
+                relay_on(t).wait_recv()
+                if chip == 0:
+                    relay_on(t).start()
+                else:
+                    grads[chip, t] += relay[t // 2]
+            by_parity(t, None, relayed)
+
     def reduce_step(t):
-        for d in merged:
-            inbox_wait(0, t)
-            grads[d, t] += inbox[0, t]
-            send_sum(d, t).start()
+        merge(t)
         total = grads[chip, t]
-        if n_own >= 1:
-            inbox_wait(1, t)
-            total = total + inbox[1, t]
-        if n_own == 2:
-            inbox_wait(0, t)
-            total = total + inbox[0, t]
+        for slot in OWN_SLOTS[chip]:
+            inbox_wait(slot, t)
+            total = total + inbox[slot, t]
         block = (2, c_len, d_head)
         kv[chip, t, 0] = (total[0] * scale).astype(jnp.bfloat16).reshape(block)
         kv[chip, t, 1] = total[1].astype(jnp.bfloat16).reshape(block)
         for c in grad_outs(t):
             c.start()
 
-    lag = LAG * (last - chip)
+    lag = LAGS[chip]
+    bufs = (pbs, dss, rows_buf)
+    for ref in bufs:
+        ref[...] = jnp.zeros(ref.shape, ref.dtype)
 
     def prologue(t, _):
         issue(t)
@@ -221,32 +301,42 @@
         for src in range(chip):
             if src not in fwd_srcs:
                 kv_wait(src, t)
-        attend(chip, t, grp, qd, kv, kvt, grads)
+        attend(chip, t, grp, qd, kv, kvt, grads, bufs, send_now)
         for c in outs(t):
             c.start()
-        for d in unmerged[::-1]:
-            send_sum(d, t).start()
+
         @pl.when(t >= lag)
         def _():
             reduce_step(t - lag)
         return 0
 
     lax.fori_loop(0, nb, step, 0)
+    for part in grad_parts(chip, 1, nb - 1, bufs, grads):
+        part()
+    send_now(nb - 1)
 
     def tail(t, _):
         reduce_step(t)
         return 0
 
-    if lag:
-        lax.fori_loop(nb - lag, nb, tail, 0)
+    lax.fori_loop(nb - lag, nb, tail, 0)
 
     def drain(t, _):
         for c in pair_copies(t, core) + kv_pushes(t):
             c.wait_send()
         for i in range(len(fwd_srcs)):
             forward(i, t).wait_send()
-        for d in range(chip):
-            send_sum(d, t).wait_send()
+        def sent(now, merged, parity):
+            routes = now + ((merged,) if merged else ())
+            relays = chip == 0 and parity == 1
+
+            def wait():
+                for route in routes:
+                    send_sum(route, t).wait_send()
+                if relays:
+                    relay_on(t).wait_send()
+            return wait if routes or relays else None
+        by_parity(t, *(sent(NOW[chip][i], MERGED[chip][i], i) for i in range(2)))
         b = (1 - core) * nb + t
         for local, away in (outs(t), grad_outs(t)):
             local.wait()
@@ -298,9 +388,13 @@
                 pltpu.VMEM((pairs, 2, d_head, 2 * c_len), jnp.bfloat16),
                 pltpu.VMEM((pairs, nb, 2, 2 * c_len, d_head), jnp.float32),
                 pltpu.VMEM((2, nb, 2, 2 * c_len, d_head), jnp.float32),
+                pltpu.VMEM((nb // 2, 2, 2 * c_len, d_head), jnp.float32),
+                pltpu.VMEM((2, pairs, 2 * c_len, CHUNK), jnp.bfloat16),
+                pltpu.VMEM((2, pairs, 2 * c_len, CHUNK), jnp.bfloat16),
+                pltpu.VMEM((2, 2, CHUNK, d_head), jnp.bfloat16),
                 dma((3, nb)), dma((3, nb)), dma((3, nb)),
                 dma((2, 2, nb)), dma((pairs, 2, nb)), dma((max(pairs - 2, 1), nb)),
-                dma((pairs, nb)), dma((2, nb)),
+                dma((pairs, nb)), dma((2, nb)), dma((nb // 2,)), dma((nb // 2,)),
                 dma((nb,)), dma((nb,)), dma((nb,)),
                 dma((nb,)), dma((nb,)), dma((nb,)),
             ],

time: 248 us -> 215 us (0.87)
  Pallas kernels: 225 us -> 194 us
    pallas_call x1, Pallas kernels: 225 us -> 194 us  [local_step(): pl.pallas_call(functools.partial(kernel, n_chip, n_q), in_specs=[any_spec...]
where the time goes in v2:
time: 215 us; the launch traced here: 212 us
  Pallas kernels  194 us (90%)
  local copies, waits for them, and re-layouts  13.4 us (6%)
  other arithmetic  3.07 us (1%)
    pallas_call x1, Pallas kernels, local_step(): pl.pallas_call(functools.partial(kernel, n_chip, n_q), in_specs=[any_spec...  194 us
    another operation x1, local copies, waits for them, and re-layouts, local_step(): odq[:, 1].reshape(shape)  11.8 us

profile of v2, /device:TPU:113, one launch (start us, length us, event | category | flops | bytes accessed | tf_op | source)
XLA Modules:
  0.0 211.5 jit_solution(1107516758612547823)
XLA Ops:
  0.6 3.1 %pad_maximum_fusion.refs_2_ = bf16[32,2,128,128]{3,2,1,0:T(8,128)(2,1)} fusion(bf16[32,1,128,128]{3,2,1,0:T(8,128)(2,1)} %bitcast.16, bf16[32,1,128,128]{3,2,1,0:T(8,128)(2,1)} %bitcast.17), kind=kLoop, calls=%fused_computation.2 | loop fusion | flops 1048576 | bytes 4194304 | tf_op jit(solution)/shard_map/stack | solution.py:374
  3.7 194.4 %shard_map.75 = (bf16[32,2,1024,128]{3,2,1,0:T(8,128)(2,1)}, bf16[32,2,128,128]{3,2,1,0:T(8,128)(2,1)}) custom-call(bf16[32,1024,128]{2,1,0:T(8,128)(2,1)} %bitcast.18, bf16[32,1024,128]{2,1,0:T(8,128)(2,1)} %bitcast.19, bf16[32,2,128,128]{3,2,1,0:T(8,128)(2,1)} %pad_maximum_fusion.refs_2_), custom_call_target="tpu_custom_call" | custom-call | flops 51539607552 | bytes 33554432 | tf_op jit(solution)/shard_map/pallas_call | solution.py:379
  198.1 0.0 copy-start
  198.1 11.8 %slice_bitcast_fusion = (bf16[32,128,8,128]{3,2,1,0:T(8,128)(2,1)}, bf16[32,128,8,128]{3,2,1,0:T(8,128)(2,1)}) fusion(bf16[32,2,1024,128]{3,2,1,0:T(8,128)(2,1)} %get-tuple-element.6), kind=kLoop, calls=%fused_computation | loop fusion | bytes 33554432 | tf_op jit(solution)/shard_map/reshape;squeeze | solution.py:405
  209.9 0.0 copy-done
  209.9 1.6 slice_bitcast_fusion.2
Async XLA Ops:
  198.1 11.8 %copy-start = (bf16[32,2,128,128]{3,2,1,0:T(8,128)(2,1)S(1)}, bf16[32,2,128,128]{3,2,1,0:T(8,128)(2,1)}, u32[]{:S(2)}) copy-start(bf16[32,2,128,128]{3,2,1,0:T(8,128)(2,1)} %get-tuple-element.7) | copy-start | bytes 6291460

commit v3 on v2

--- a/solution.py
+++ b/solution.py
@@ -11,8 +11,8 @@
 NEG_BIG = -1e30
 CHUNK = 512
 EARLY = 2
-AHEAD = 3
-FORWARD = 2
+AHEAD = 2
+FORWARD = 1
 NT = (((1,), (1,)), ((), ()))
 
 
@@ -65,6 +65,7 @@
     mk = m * k2
     p = []
     l = 0.0
+    o_t = None
     for j in range(n):
         parts = []
         for a in range(0, span[j], c_len):
@@ -74,17 +75,14 @@
             if fill:
                 fill.pop(0)()
         p.append(parts)
+        x = [x.astype(jnp.bfloat16) for x in parts]
+        part = mm(kvt[j, 1, :, :span[j]], jnp.concatenate(x, axis=0) if len(x) > 1 else x[0])
+        o_t = part if o_t is None else o_t + part
     for step in fill:
         step()
     rl = 1.0 / l
-    o_t = None
-    for j in range(n):
-        for i, x in enumerate(p[j]):
-            pbs[half, j, i * c_len:(i + 1) * c_len] = (x * rl).astype(jnp.bfloat16)
-        part = mm(kvt[j, 1, :, :span[j]], pbs[half, j, :span[j]])
-        o_t = part if o_t is None else o_t + part
     dps = [mm_nt(vals[a:a + w], do) for a, w in list(zip(tops, span))[:EARLY]]
-    o_t = o_t.astype(jnp.bfloat16)
+    o_t = (o_t * rl).astype(jnp.bfloat16)
     delta = jnp.sum(do.T.astype(jnp.float32) * o_t.astype(jnp.float32), axis=0, keepdims=True)
     dq_t = None
     for j in range(n):
@@ -93,7 +91,9 @@
             dps.append(mm_nt(vals[a:a + span[j + EARLY]], do))
         for i, x in enumerate(p[j]):
             at = slice(i * c_len, (i + 1) * c_len)
-            dss[half, j, at] = (x * rl * (dps[j][at] - delta)).astype(jnp.bfloat16)
+            x = x * rl
+            pbs[half, j, at] = x.astype(jnp.bfloat16)
+            dss[half, j, at] = (x * (dps[j][at] - delta)).astype(jnp.bfloat16)
         part = mm(kvt[j, 0, :, :span[j]], dss[half, j, :span[j]])
         dq_t = part if dq_t is None else dq_t + part
     qd[t, half, 0, rs] = o_t.T
@@ -125,14 +125,16 @@
     lax.fori_loop(0, qd.shape[-2] // CHUNK, chunk, 0)
 
 
-NOW = {0: ((), ()), 1: (((0, 0, 1),), ()), 2: (((0, 3, 0),), ((1, 1, 1), (0, 1, 0))),
-       3: (((1, 2, 0), (2, 2, 1)), ((1, 0, 2), (0, 0, 0), (2, 2, 1)))}
-MERGED = {0: (None, None), 1: (None, (0, 0, 1)), 2: ((1, 1, 1), None), 3: ((0, 0, 0), None)}
+RELAY = 2
+NOW = {0: (), 1: ((0, 0, 0, 1),), 2: ((0, 0, 3, 0), (0, 1, 1, 0), (1, 1, 1, 1)),
+       3: ((1, 0, 2, 0), (1, 1, 0, RELAY), (2, 0, 2, 1), (0, 1, 0, 0), (2, 1, 2, 1))}
+MERGED = {0: None, 1: (0, 1, 0, 1), 2: (1, 0, 1, 1), 3: (0, 0, 0, 0)}
 OWN_SLOTS = {0: (1, 0), 1: (1,), 2: (1,), 3: ()}
-LAGS = {0: 7, 1: 5, 2: 3, 3: 3}
-
-
-def run_chip(chip, n_chip, grp, q_ref, do_ref, kv_ref, odq_ref, dkv_ref, qd, kv, kvt, grads, inbox, relay,
+LAGS = {0: 6, 1: 4, 2: 2, 3: 2}
+RELAY_LAG = 3
+
+
+def run_chip(chip, n_chip, grp, q_ref, do_ref, k_ref, v_ref, odq_ref, dkv_ref, qd, kv, kvt, grads, inbox, relay,
              pbs, dss, rows_buf, load_sem, pair_send, pair_recv, kv_send, kv_recv, fwd_send, sum_send, sum_recv,
              relay_send, relay_recv,
              out_sem, out_send, out_recv, g_sem, g_send, g_recv):
@@ -158,22 +160,25 @@
         b = core * nb + t
         return [pltpu.make_async_copy(q_ref.at[b], qd.at[t, core, 0], load_sem.at[0, t]),
                 pltpu.make_async_copy(do_ref.at[b], qd.at[t, core, 1], load_sem.at[1, t]),
-                pltpu.make_async_copy(kv_ref.at[b], kv.at[chip, t, :, core], load_sem.at[2, t])]
+                pltpu.make_async_copy(k_ref.at[b], kv.at[chip, t, 0, core], load_sem.at[2, t]),
+                pltpu.make_async_copy(v_ref.at[b], kv.at[chip, t, 1, core], load_sem.at[3, t])]
 
     def pair_copies(t, half):
         b = (1 - core) * nb + t
         to = dev(chip, 1 - core)
         return [remote(q_ref.at[b], qd.at[t, half, 0], pair_send.at[0, t], pair_recv.at[0, t], to),
                 remote(do_ref.at[b], qd.at[t, half, 1], pair_send.at[1, t], pair_recv.at[1, t], to),
-                remote(kv_ref.at[b], kv.at[chip, t, :, half], pair_send.at[2, t], pair_recv.at[2, t], to)]
+                remote(k_ref.at[b], kv.at[chip, t, 0, half], pair_send.at[2, t], pair_recv.at[2, t], to),
+                remote(v_ref.at[b], kv.at[chip, t, 1, half], pair_send.at[3, t], pair_recv.at[3, t], to)]
 
     def kv_pushes(t):
         out = []
         for i, to_chip in enumerate(targets):
             for other in range(2):
                 plane = core if other == 0 else 1 - core
-                out.append(remote(kv_ref.at[plane * nb + t], kv.at[chip, t, :, core], kv_send.at[i, other, t],
-                                  kv_recv.at[chip, core, t], dev(to_chip, plane)))
+                for w, ref in enumerate((k_ref, v_ref)):
+                    out.append(remote(ref.at[plane * nb + t], kv.at[chip, t, w, core], kv_send.at[i, other, w, t],
+                                      kv_recv.at[chip, core, w, t], dev(to_chip, plane)))
         return out
 
     def direct(src):
@@ -182,16 +187,17 @@
     def kv_wait(src, t):
         if direct(src):
             for half in range(2):
-                remote(kv_ref.at[0], kv.at[src, t, :, half], kv_send.at[0, 0, t], kv_recv.at[src, half, t],
-                       dev(chip, 1 - core)).wait_recv()
+                for w in range(2):
+                    remote(k_ref.at[0], kv.at[src, t, w, half], kv_send.at[0, 0, w, t], kv_recv.at[src, half, w, t],
+                           dev(chip, 1 - core)).wait_recv()
         else:
-            remote(kv.at[src, t], kv.at[src, t], fwd_send.at[0, t], kv_recv.at[src, 0, t], dev(chip, 1 - core)).wait_recv()
+            remote(kv.at[src, t], kv.at[src, t], fwd_send.at[0, t], kv_recv.at[src, 0, 0, t], dev(chip, 1 - core)).wait_recv()
 
     fwd_srcs = [s for s in range(chip) if chip < last and not (s == 0 and chip + 1 == last)]
 
     def forward(i, t):
         src = fwd_srcs[i]
-        return remote(kv.at[src, t], kv.at[src, t], fwd_send.at[i, t], kv_recv.at[src, 0, t], dev(chip + 1, core))
+        return remote(kv.at[src, t], kv.at[src, t], fwd_send.at[i, t], kv_recv.at[src, 0, 0, t], dev(chip + 1, core))
 
     def issue(t):
         for c in loads(t) + pair_copies(t, core) + kv_pushes(t):
@@ -203,25 +209,19 @@
             forward(i, t).start()
 
     def send_sum(route, t):
-        d, to_chip, slot = route
-        if slot == 2:
-            dst, recv = relay.at[t // 2], relay_recv.at[t // 2]
+        d, w, to_chip, slot = route
+        if slot == RELAY:
+            dst, recv = relay.at[t], relay_recv.at[t]
         else:
-            dst, recv = inbox.at[slot, t], sum_recv.at[slot, t]
-        return remote(grads.at[d, t], dst, sum_send.at[d, t], recv, dev(to_chip, core))
+            dst, recv = inbox.at[slot, t, w], sum_recv.at[slot, w, t]
+        return remote(grads.at[d, t, w], dst, sum_send.at[d, w, t], recv, dev(to_chip, core))
 
     def relay_on(t):
-        u = t // 2
-        return remote(relay.at[u], relay.at[u], relay_send.at[u], relay_recv.at[u], dev(1, core))
-
-    def inbox_wait(slot, t):
-        remote(inbox.at[slot, t], inbox.at[slot, t], sum_send.at[0, t], sum_recv.at[slot, t],
-               dev(chip, 1 - core)).wait_recv()
-
-    def by_parity(t, even, odd):
-        for parity, body in enumerate((even, odd)):
-            if body is not None:
-                pl.when(t % 2 == parity)(body)
+        return remote(relay.at[t], relay.at[t], relay_send.at[t], relay_recv.at[t], dev(1, core))
+
+    def inbox_wait(slot, w, t):
+        ref = inbox.at[slot, t, w]
+        remote(ref, ref, sum_send.at[0, w, t], sum_recv.at[slot, w, t], dev(chip, 1 - core)).wait_recv()
 
     def outs(t):
         b = core * nb + t
@@ -234,36 +234,27 @@
                 remote(kv.at[chip, t, :, 1 - core], dkv_ref.at[b], g_send.at[t], g_recv.at[t], dev(chip, 1 - core))]
 
     def send_now(t):
-        def body(routes):
-            def start():
-                for route in routes:
-                    send_sum(route, t).start()
-            return start if routes else None
-        by_parity(t, *map(body, NOW[chip]))
-
-    def merge(t):
-        def body(route):
-            def pass_on():
-                inbox_wait(0, t)
-                grads[route[0], t] += inbox[0, t]
-                send_sum(route, t).start()
-            return pass_on if route else None
-        by_parity(t, *map(body, MERGED[chip]))
-        if chip < 2:
-            def relayed():
-                relay_on(t).wait_recv()
-                if chip == 0:
-                    relay_on(t).start()
-                else:
-                    grads[chip, t] += relay[t // 2]
-            by_parity(t, None, relayed)
+        for route in NOW[chip]:
+            send_sum(route, t).start()
+
+    def pass_relay(t):
+        relay_on(t).wait_recv()
+        relay_on(t).start()
 
     def reduce_step(t):
-        merge(t)
-        total = grads[chip, t]
+        if MERGED[chip]:
+            d, w = MERGED[chip][:2]
+            inbox_wait(0, w, t)
+            grads[d, t, w] += inbox[0, t, w]
+            send_sum(MERGED[chip], t).start()
+        total = [grads[chip, t, 0], grads[chip, t, 1]]
         for slot in OWN_SLOTS[chip]:
-            inbox_wait(slot, t)
-            total = total + inbox[slot, t]
+            for w in range(2):
+                inbox_wait(slot, w, t)
+                total[w] = total[w] + inbox[slot, t, w]
+        if chip == 1:
+            relay_on(t).wait_recv()
+            total[1] = total[1] + relay[t]
         block = (2, c_len, d_head)
         kv[chip, t, 0] = (total[0] * scale).astype(jnp.bfloat16).reshape(block)
         kv[chip, t, 1] = total[1].astype(jnp.bfloat16).reshape(block)
@@ -305,6 +296,11 @@
         for c in outs(t):
             c.start()
 
+        if chip == 0:
+            @pl.when(t >= RELAY_LAG)
+            def _():
+                pass_relay(t - RELAY_LAG)
+
         @pl.when(t >= lag)
         def _():
             reduce_step(t - lag)
@@ -314,6 +310,13 @@
     for part in grad_parts(chip, 1, nb - 1, bufs, grads):
         part()
     send_now(nb - 1)
+
+    def relay_tail(t, _):
+        pass_relay(t)
+        return 0
+
+    if chip == 0:
+        lax.fori_loop(nb - RELAY_LAG, nb, relay_tail, 0)
 
     def tail(t, _):
         reduce_step(t)
@@ -326,17 +329,10 @@
             c.wait_send()
         for i in range(len(fwd_srcs)):
             forward(i, t).wait_send()
-        def sent(now, merged, parity):
-            routes = now + ((merged,) if merged else ())
-            relays = chip == 0 and parity == 1
-
-            def wait():
-                for route in routes:
-                    send_sum(route, t).wait_send()
-                if relays:
-                    relay_on(t).wait_send()
-            return wait if routes or relays else None
-        by_parity(t, *(sent(NOW[chip][i], MERGED[chip][i], i) for i in range(2)))
+        for route in NOW[chip] + ((MERGED[chip],) if MERGED[chip] else ()):
+            send_sum(route, t).wait_send()
+        if chip == 0:
+            relay_on(t).wait_send()
         b = (1 - core) * nb + t
         for local, away in (outs(t), grad_outs(t)):
             local.wait()
@@ -371,14 +367,15 @@
         nb = n_batch // 2
         q = queries.reshape(n_batch, rows, d_head)
         do = grad_out.reshape(n_batch, rows, d_head)
-        kv = jnp.stack([keys.reshape(n_batch, c_len, d_head), values.reshape(n_batch, c_len, d_head)], axis=1)
+        k = keys.reshape(n_batch, c_len, d_head)
+        v = values.reshape(n_batch, c_len, d_head)
         dma = pltpu.SemaphoreType.DMA
         any_spec = pl.BlockSpec(memory_space=pl.ANY)
         pairs = n_chip
         flops = 2 * nb * 2 * rows * n_chip * 2 * c_len * d_head * 6
         odq, dkv = pl.pallas_call(
             functools.partial(kernel, n_chip, n_q),
-            in_specs=[any_spec] * 3,
+            in_specs=[any_spec] * 4,
             out_specs=[any_spec] * 2,
             out_shape=[jax.ShapeDtypeStruct((n_batch, 2, rows, d_head), jnp.bfloat16),
                        jax.ShapeDtypeStruct((n_batch, 2, c_len, d_head), jnp.bfloat16)],
@@ -388,19 +385,19 @@
                 pltpu.VMEM((pairs, 2, d_head, 2 * c_len), jnp.bfloat16),
                 pltpu.VMEM((pairs, nb, 2, 2 * c_len, d_head), jnp.float32),
                 pltpu.VMEM((2, nb, 2, 2 * c_len, d_head), jnp.float32),
-                pltpu.VMEM((nb // 2, 2, 2 * c_len, d_head), jnp.float32),
+                pltpu.VMEM((nb, 2 * c_len, d_head), jnp.float32),
                 pltpu.VMEM((2, pairs, 2 * c_len, CHUNK), jnp.bfloat16),
                 pltpu.VMEM((2, pairs, 2 * c_len, CHUNK), jnp.bfloat16),
                 pltpu.VMEM((2, 2, CHUNK, d_head), jnp.bfloat16),
-                dma((3, nb)), dma((3, nb)), dma((3, nb)),
-                dma((2, 2, nb)), dma((pairs, 2, nb)), dma((max(pairs - 2, 1), nb)),
-                dma((pairs, nb)), dma((2, nb)), dma((nb // 2,)), dma((nb // 2,)),
+                dma((4, nb)), dma((4, nb)), dma((4, nb)),
+                dma((2, 2, 2, nb)), dma((pairs, 2, 2, nb)), dma((max(pairs - 2, 1), nb)),
+                dma((pairs, 2, nb)), dma((2, 2, nb)), dma((nb,)), dma((nb,)),
                 dma((nb,)), dma((nb,)), dma((nb,)),
                 dma((nb,)), dma((nb,)), dma((nb,)),
             ],
             compiler_params=pltpu.CompilerParams(vmem_limit_bytes=67043328, collective_id=0, has_side_effects=True),
             cost_estimate=pl.CostEstimate(flops=flops, bytes_accessed=4 * q.size * 2, transcendentals=0),
-        )(q, do, kv)
+        )(q, do, k, v)
         shape, kv_shape = queries.shape, keys.shape
         return (odq[:, 0].reshape(shape), odq[:, 1].reshape(shape),
                 dkv[:, 0].reshape(kv_shape), dkv[:, 1].reshape(kv_shape))

time: 215 us -> 191 us (0.89); the launches traced: 212 us -> 191 us
  Pallas kernels: 194 us -> 177 us
  other arithmetic: 3.07 us -> 0 us
    pallas_call x1, Pallas kernels: 194 us -> 177 us  [local_step(): pl.pallas_call(functools.partial(kernel, n_chip, n_q), in_specs=[any_spec...]
    another operation x1 -> x0, other arithmetic: 3.07 us -> none  [local_step(): jnp.stack([keys.reshape(n_batch, c_len, d_head), values.reshape(n_batch,...]
where the time goes in v3:
time: 191 us
  Pallas kernels  177 us (93%)
  local copies, waits for them, and re-layouts  13.4 us (7%)
    pallas_call x1, Pallas kernels, local_step(): pl.pallas_call(functools.partial(kernel, n_chip, n_q), in_specs=[any_spec...  177 us
    another operation x1, local copies, waits for them, and re-layouts, local_step(): odq[:, 1].reshape(shape)  11.8 us

profile of v3, /device:TPU:113, one launch (start us, length us, event | category | flops | bytes accessed | tf_op | source)
XLA Modules:
  0.0 190.7 jit_solution(17784282421443207302)
XLA Ops:
  0.6 176.7 %shard_map.75 = (bf16[32,2,1024,128]{3,2,1,0:T(8,128)(2,1)}, bf16[32,2,128,128]{3,2,1,0:T(8,128)(2,1)}) custom-call(bf16[32,1024,128]{2,1,0:T(8,128)(2,1)} %bitcast.16, bf16[32,1024,128]{2,1,0:T(8,128)(2,1)} %bitcast.17, bf16[32,128,128]{2,1,0:T(8,128)(2,1)} %bitcast.18, bf16[32,128,128]{2,1,0:T(8,128)(2,1)} %bitcast.19), custom_call_target="tpu_custom_call" | custom-call | flops 51539607552 | bytes 33554432 | tf_op jit(solution)/shard_map/pallas_call | solution.py:376
  177.3 0.0 copy-start
  177.3 11.8 %slice_bitcast_fusion = (bf16[32,128,8,128]{3,2,1,0:T(8,128)(2,1)}, bf16[32,128,8,128]{3,2,1,0:T(8,128)(2,1)}) fusion(bf16[32,2,1024,128]{3,2,1,0:T(8,128)(2,1)} %get-tuple-element.6), kind=kLoop, calls=%fused_computation | loop fusion | bytes 33554432 | tf_op jit(solution)/shard_map/reshape;squeeze | solution.py:402
  189.1 0.0 copy-done
  189.1 1.6 slice_bitcast_fusion.2
Async XLA Ops:
  177.3 11.8 %copy-start = (bf16[32,2,128,128]{3,2,1,0:T(8,128)(2,1)S(1)}, bf16[32,2,128,128]{3,2,1,0:T(8,128)(2,1)}, u32[]{:S(2)}) copy-start(bf16[32,2,128,128]{3,2,1,0:T(8,128)(2,1)} %get-tuple-element.7) | copy-start | bytes 6291460

commit v4 on v3

--- a/solution.py
+++ b/solution.py
@@ -46,7 +46,7 @@
     k2 = scale * math.log2(math.e)
     n = chip + 1
     fill = list(fill)
-    rs = pl.ds(pl.multiple_of(r * CHUNK, CHUNK), CHUNK)
+    rs = pl.ds(r * CHUNK, CHUNK)
     q = qd[t, half, 0, rs]
     do = qd[t, half, 1, rs]
     rows_buf[half, 0] = q
@@ -109,20 +109,25 @@
         kvt[j, 1] = kv[j, t, 1].reshape(pair, d_head).T
         grads[j, t] = jnp.zeros(grads.shape[2:], jnp.float32)
 
-    def chunk(r, _):
-        before = jnp.where(r == 0, jnp.maximum(t - 1, 0), t)
-        softmax_part(chip, 0, r, t, grp, qd, kv, kvt, bufs, grad_parts(chip, 1, before, bufs, grads))
-
-        @pl.when((r == 0) & (t >= 1))
-        def _():
-            send_now(t - 1)
-
+    def second(r):
         @pl.when(t < nb)
         def _():
             softmax_part(chip, 1, r, t, grp, qd, kv, kvt, bufs, grad_parts(chip, 0, t, bufs, grads))
-        return 0
-
-    lax.fori_loop(0, qd.shape[-2] // CHUNK, chunk, 0)
+
+    def first(r):
+        before = jnp.maximum(t - 1, 0) if r == 0 else t
+        softmax_part(chip, 0, r, t, grp, qd, kv, kvt, bufs, grad_parts(chip, 1, before, bufs, grads))
+
+    first(0)
+
+    @pl.when(t >= 1)
+    def _():
+        send_now(t - 1)
+
+    second(0)
+    for r in range(1, qd.shape[-2] // CHUNK):
+        pl.when(t < nb)(functools.partial(first, r))
+        second(r)
 
 
 RELAY = 2
@@ -263,8 +268,6 @@
 
     lag = LAGS[chip]
     bufs = (pbs, dss, rows_buf)
-    for ref in bufs:
-        ref[...] = jnp.zeros(ref.shape, ref.dtype)
 
     def prologue(t, _):
         issue(t)
@@ -276,6 +279,9 @@
             issue_forward(t)
             return 0
         lax.fori_loop(0, FORWARD, fwd_prologue, 0)
+
+    for ref in bufs:
+        ref[...] = jnp.zeros(ref.shape, ref.dtype)
 
     def step(t, _):
         @pl.when(t + AHEAD < nb)

time: 191 us -> 187 us (0.979)
  Pallas kernels: 177 us -> 173 us
    pallas_call x1, Pallas kernels: 177 us -> 173 us  [local_step(): pl.pallas_call(functools.partial(kernel, n_chip, n_q), in_specs=[any_spec...]
where the time goes in v4:
time: 187 us
  Pallas kernels  173 us (93%)
  local copies, waits for them, and re-layouts  13.4 us (7%)
    pallas_call x1, Pallas kernels, local_step(): pl.pallas_call(functools.partial(kernel, n_chip, n_q), in_specs=[any_spec...  173 us
    another operation x1, local copies, waits for them, and re-layouts, local_step(): odq[:, 1].reshape(shape)  11.8 us

profile of v4, /device:TPU:113, one launch (start us, length us, event | category | flops | bytes accessed | tf_op | source)
XLA Modules:
  0.0 186.8 jit_solution(7609791627710006121)
XLA Ops:
  0.6 172.7 %shard_map.75 = (bf16[32,2,1024,128]{3,2,1,0:T(8,128)(2,1)}, bf16[32,2,128,128]{3,2,1,0:T(8,128)(2,1)}) custom-call(bf16[32,1024,128]{2,1,0:T(8,128)(2,1)} %bitcast.16, bf16[32,1024,128]{2,1,0:T(8,128)(2,1)} %bitcast.17, bf16[32,128,128]{2,1,0:T(8,128)(2,1)} %bitcast.18, bf16[32,128,128]{2,1,0:T(8,128)(2,1)} %bitcast.19), custom_call_target="tpu_custom_call" | custom-call | flops 51539607552 | bytes 33554432 | tf_op jit(solution)/shard_map/pallas_call | solution.py:382
  173.4 0.0 copy-start
  173.4 11.8 %slice_bitcast_fusion = (bf16[32,128,8,128]{3,2,1,0:T(8,128)(2,1)}, bf16[32,128,8,128]{3,2,1,0:T(8,128)(2,1)}) fusion(bf16[32,2,1024,128]{3,2,1,0:T(8,128)(2,1)} %get-tuple-element.6), kind=kLoop, calls=%fused_computation | loop fusion | bytes 33554432 | tf_op jit(solution)/shard_map/reshape;squeeze | solution.py:408
  185.2 0.0 copy-done
  185.2 1.6 slice_bitcast_fusion.2
Async XLA Ops:
  173.4 11.8 %copy-start = (bf16[32,2,128,128]{3,2,1,0:T(8,128)(2,1)S(1)}, bf16[32,2,128,128]{3,2,1,0:T(8,128)(2,1)}, u32[]{:S(2)}) copy-start(bf16[32,2,128,128]{3,2,1,0:T(8,128)(2,1)} %get-tuple-element.7) | copy-start | bytes 6291460
